TPU v7x, 256 devices: a whole 4x4x8 slice. The times are simulated.
256 devices in a mesh: dom: 32 (over x, y, core), feat: 8 (over z).
Axes of the slice: x: 4, y: 4, z: 8, core: 2. Of those that a mesh axis runs over, the one named last changes fastest.
Arguments:
- features: bfloat16 [512, 262144], P('feat', 'dom'), may hold values from -3 to 3
- send_blocks: int32 [32, 32, 8], P('dom'), may hold values from 0 to 63, as said below
- counts: int32 [32, 32], P('dom'), may hold values from 0 to 8, as said below
- tile_blocks: int32 [24, 2048], P(None, 'dom'), may hold values from 0 to 319, as said below
- neighbours: int32 [24, 262144], P(None, 'dom'), may hold values from 0 to 127
- degree: int32 [262144], P('dom'), may hold values from 1 to 24
- epsilon: float32 [1], replicated, may hold values from -0.3 to 0.6
- w_first: bfloat16 [512, 512], replicated, may hold values from -0.25 to 0.25
- b_first: float32 [512], replicated, may hold values from -3 to 3
- w_second: bfloat16 [512, 512], replicated, may hold values from -0.25 to 0.25
- b_second: float32 [512], replicated, may hold values from -3 to 3
Outputs:
- updated: bfloat16 [262144, 512], P(('dom', 'feat'))
Inputs may be any that keep to these rules, and one draw needn't show every extreme that they name: `send_blocks`: entry [q, p, s] is a row block of partition q; the entries of one pair (q, p) are distinct. counts[q, p] leading slots of send_blocks[q, p] are used; zero where q == p; in every draw some partition receives 8 blocks from every other partition. `tile_blocks`: an entry for a row block of partition p is below 64 (a row block of p) or equals 64 + q * 8 + s for a slot s of a partition q other than p.
All inputs are finite; a program needn't handle non-finite values.
Results may differ from a plain program's by a relative error of at most 0.0055.
Values may be sent and summed in bfloat16 or wider, within the bound.
A program may use at most 64 MiB of HBM per device.

v0:
```python
import jax
import jax.numpy as jnp
from jax import lax
from jax.sharding import PartitionSpec as P

BLOCK = 128


def over_tiles(table, tiles, offsets, weight):
    width, block_count = tiles.shape
    col_count = table.shape[1]
    block_size = table.shape[2]
    group = min(block_count, 16)
    steps = block_count // group
    tile_steps = tiles.reshape(width, steps, group).transpose(1, 0, 2)
    offset_steps = offsets.reshape(width, steps, group, block_size).transpose(1, 0, 2, 3)
    weight_steps = weight.reshape(width, steps, group, block_size).transpose(1, 0, 2, 3)
    source_ids = jnp.arange(block_size, dtype=jnp.int32)[:, None]

    def one_step(triple):
        gathered = table[triple[0]]
        onehot = jnp.where(
            triple[1][:, :, None, :] == source_ids,
            triple[2][:, :, None, :],
            jnp.zeros((), jnp.bfloat16),
        )
        return jnp.einsum("kgcs,kgsd->gcd", gathered, onehot, preferred_element_type=jnp.float32)

    result = lax.map(one_step, (tile_steps, offset_steps, weight_steps))
    return result.reshape(block_count, col_count, block_size)


def per_device(
    features,
    send_blocks,
    counts,
    tile_blocks,
    neighbours,
    degree,
    epsilon,
    w_first,
    b_first,
    w_second,
    b_second,
):
    col_count, row_count = features.shape
    part_count = lax.axis_size("dom")
    slot_count = send_blocks.shape[2]
    list_width = neighbours.shape[0]
    block_count = row_count // BLOCK
    feat_blocks = features.reshape(col_count, block_count, BLOCK).transpose(1, 0, 2)
    chosen = feat_blocks[send_blocks[0]]
    slot_used = jnp.arange(slot_count, dtype=jnp.int32)[None, :] < counts[0][:, None]
    chosen = jnp.where(slot_used[:, :, None, None], chosen, jnp.zeros_like(chosen))
    arrived = lax.all_to_all(chosen, "dom", split_axis=0, concat_axis=0, tiled=True).reshape(
        part_count * slot_count, col_count, BLOCK
    )
    live_mask = jnp.arange(list_width, dtype=jnp.int32)[:, None] < degree[None, :]
    halo_table = jnp.concatenate([feat_blocks, arrived], axis=0)
    near_blocks = over_tiles(halo_table, tile_blocks, neighbours, live_mask.astype(jnp.bfloat16))
    near_sum = near_blocks.transpose(1, 0, 2).reshape(col_count, row_count)
    mixed = ((1.0 + epsilon[0]) * features.astype(jnp.float32) + near_sum).astype(jnp.bfloat16)
    groups = lax.axis_size("feat")
    owned_rows = row_count // groups
    group_rows = min(owned_rows, 512)
    shaped = mixed.reshape(col_count, groups, owned_rows // group_rows, group_rows)
    parcel = lax.all_to_all(shaped, "feat", split_axis=1, concat_axis=0, tiled=True)
    flat_cols = parcel.reshape(parcel.shape[0], -1)
    pre_act = (
        lax.dot_general(
            flat_cols, w_first, (((0,), (0,)), ((), ())), preferred_element_type=jnp.float32
        )
        + b_first
    )
    activated = jax.nn.relu(pre_act).astype(jnp.bfloat16)
    return (jnp.dot(activated, w_second, preferred_element_type=jnp.float32) + b_second).astype(
        jnp.bfloat16
    )


def solution(mesh):
    return jax.shard_map(
        per_device,
        mesh=mesh,
        in_specs=(
            P("feat", "dom"),
            P("dom", None, None),
            P("dom", None),
            P(None, "dom"),
            P(None, "dom"),
            P("dom"),
            P(),
            P(),
            P(),
            P(),
            P(),
        ),
        out_specs=P(("dom", "feat"), None),
        check_vma=False,
    )
```

profile of v0, /device:TPU:1, one launch (start us, length us, event | category | flops | bytes accessed | tf_op | source)
XLA Modules:
  0.0 166.9 jit_solution(42159184915654737)
XLA Ops:
  0.0 1.6 bitcast_bitcast_fusion
  3.2 3.0 %gather_fusion.1 = bf16[256,64,128]{2,1,0:T(8,128)(2,1)} fusion(bf16[64,64,128]{2,1,0:T(8,128)(2,1)S(1)} %bitcast_bitcast_fusion, s32[1024]{0:T(1024)S(1)} %pad_clamp_fusion.1), kind=kCustom, calls=%fused_computation.1 | custom fusion | bytes 8389632 | tf_op jit(solution)/shard_map/gather | solution.py:52
  6.2 3.8 %broadcast_select_fusion = bf16[32,8,64,128]{3,2,1,0:T(8,128)(2,1)} fusion(bf16[32,8,64,128]{3,2,1,0:T(8,128)(2,1)} %bitcast.72, pred[32,8]{1,0:T(8,128)(4,1)S(1)} %iota_compare_fusion.2), kind=kLoop, calls=%fused_computation.18 | loop fusion | flops 2097152 | bytes 8388864 | tf_op jit(solution)/shard_map/jit(_where)/select_n | solution.py:54
  10.0 8.8 %all-to-all-start = ((bf16[32,8,64,128]{3,2,1,0:T(8,128)(2,1)}), bf16[32,8,64,128]{3,2,1,0:T(8,128)(2,1)}, u32[]{:S(2)}, u32[]{:S(2)}) async-start(bf16[32,8,64,128]{3,2,1,0:T(8,128)(2,1)} %broadcast_select_fusion), calls=%async_computation | async-start | bytes 8388608 | tf_op jit(solution)/shard_map/all_to_all | solution.py:55
  19.7 0.8 fusion.18
  20.6 50.4 %all-to-all-done = bf16[32,8,64,128]{3,2,1,0:T(8,128)(2,1)} async-done(((bf16[32,8,64,128]{3,2,1,0:T(8,128)(2,1)}), bf16[32,8,64,128]{3,2,1,0:T(8,128)(2,1)}, u32[]{:S(2)}, u32[]{:S(2)}) %all-to-all-start) | async-done | bytes 4194336 | tf_op jit(solution)/shard_map/all_to_all | solution.py:55
  70.9 5.0 %pad_maximum_fusion = bf16[320,64,128]{2,1,0:T(8,128)(2,1)} fusion(bf16[256,64,128]{2,1,0:T(8,128)(2,1)} %bitcast.7, bf16[64,64,128]{2,1,0:T(8,128)(2,1)S(1)} %bitcast_bitcast_fusion), kind=kLoop, calls=%fused_computation.17 | loop fusion | flops 2621440 | bytes 10485760 | tf_op jit(solution)/shard_map/concatenate | solution.py:59
  75.9 49.6 %while.11 = (s32[]{:T(128)}, f32[4,16,64,128]{3,2,1,0:T(8,128)}, s32[4,24,16]{1,2,0:T(8,128)S(1)}, bf16[320,64,128]{2,1,0:T(8,128)(2,1)}, s32[4,24,16,128]{3,2,0...) while((s32[]{:T(128)}, f32[4,16,64,128]{3,2,1,0:T(8,128)}, ...), condition=%wide.region_1.2_spmd.clone, body=%wide.region_0.1_spmd.clone.sunk | while | flops 817891456 | bytes 20303448 | solution.py:29
  76.1 6.6 %gather_fusion = bf16[384,64,128]{2,1,0:T(8,128)(2,1)} fusion(bf16[320,64,128]{2,1,0:T(8,128)(2,1)} %get-tuple-element.135, s32[1024]{0:T(1024)S(1)} %pad_clamp_fusion.3), kind=kCustom, calls=%fused_computation.clone.clone.1 | custom fusion | bytes 12584448 | tf_op jit(solution)/shard_map/while/body/eval_jaxpr/gather | solution.py:21
  82.8 0.9 dynamic-slice_bitcast_fusion.5
  83.7 4.7 %fusion.30 = f32[4,16,64,128]{3,2,1,0:T(8,128)} fusion(f32[4,16,64,128]{3,2,1,0:T(8,128)} %get-tuple-element.126, s32[]{:T(128)} %get-tuple-element.125, bf16[24,16,64,128]{3,2,1,0:T(8,128)(2,1)} %bitcast.71, s32[24,16,128]{2,1,0:T(8,128)S(1)} %dynamic-slice_bitcast_fusion.4, bf16[24,16,128]{2,1,0:T(8,128)(2,1)S(1)} %dynamic-slice_bitcast_fusion.5), kind=kOutput, calls=%fused_computation.10.clone.1 | convolution fusion | flops 817889280 | bytes 7111168 | tf_op jit(solution)/shard_map/while/body/eval_jaxpr/kgcs,kgsd->gcd/dot_general | solution.py:27
  88.6 6.5 %gather_fusion = bf16[384,64,128]{2,1,0:T(8,128)(2,1)} fusion(bf16[320,64,128]{2,1,0:T(8,128)(2,1)} %get-tuple-element.135, s32[1024]{0:T(1024)S(1)} %pad_clamp_fusion.3), kind=kCustom, calls=%fused_computation.clone.clone.1 | custom fusion | bytes 12584448 | tf_op jit(solution)/shard_map/while/body/eval_jaxpr/gather | solution.py:21
  95.1 0.9 dynamic-slice_bitcast_fusion.5
  96.0 4.8 %fusion.30 = f32[4,16,64,128]{3,2,1,0:T(8,128)} fusion(f32[4,16,64,128]{3,2,1,0:T(8,128)} %get-tuple-element.126, s32[]{:T(128)} %get-tuple-element.125, bf16[24,16,64,128]{3,2,1,0:T(8,128)(2,1)} %bitcast.71, s32[24,16,128]{2,1,0:T(8,128)S(1)} %dynamic-slice_bitcast_fusion.4, bf16[24,16,128]{2,1,0:T(8,128)(2,1)S(1)} %dynamic-slice_bitcast_fusion.5), kind=kOutput, calls=%fused_computation.10.clone.1 | convolution fusion | flops 817889280 | bytes 7111168 | tf_op jit(solution)/shard_map/while/body/eval_jaxpr/kgcs,kgsd->gcd/dot_general | solution.py:27
  101.0 6.5 %gather_fusion = bf16[384,64,128]{2,1,0:T(8,128)(2,1)} fusion(bf16[320,64,128]{2,1,0:T(8,128)(2,1)} %get-tuple-element.135, s32[1024]{0:T(1024)S(1)} %pad_clamp_fusion.3), kind=kCustom, calls=%fused_computation.clone.clone.1 | custom fusion | bytes 12584448 | tf_op jit(solution)/shard_map/while/body/eval_jaxpr/gather | solution.py:21
  107.5 0.9 dynamic-slice_bitcast_fusion.5
  108.4 4.8 %fusion.30 = f32[4,16,64,128]{3,2,1,0:T(8,128)} fusion(f32[4,16,64,128]{3,2,1,0:T(8,128)} %get-tuple-element.126, s32[]{:T(128)} %get-tuple-element.125, bf16[24,16,64,128]{3,2,1,0:T(8,128)(2,1)} %bitcast.71, s32[24,16,128]{2,1,0:T(8,128)S(1)} %dynamic-slice_bitcast_fusion.4, bf16[24,16,128]{2,1,0:T(8,128)(2,1)S(1)} %dynamic-slice_bitcast_fusion.5), kind=kOutput, calls=%fused_computation.10.clone.1 | convolution fusion | flops 817889280 | bytes 7111168 | tf_op jit(solution)/shard_map/while/body/eval_jaxpr/kgcs,kgsd->gcd/dot_general | solution.py:27
  113.3 6.5 %gather_fusion = bf16[384,64,128]{2,1,0:T(8,128)(2,1)} fusion(bf16[320,64,128]{2,1,0:T(8,128)(2,1)} %get-tuple-element.135, s32[1024]{0:T(1024)S(1)} %pad_clamp_fusion.3), kind=kCustom, calls=%fused_computation.clone.clone.1 | custom fusion | bytes 12584448 | tf_op jit(solution)/shard_map/while/body/eval_jaxpr/gather | solution.py:21
  119.9 0.9 dynamic-slice_bitcast_fusion.5
  120.8 4.8 %fusion.30 = f32[4,16,64,128]{3,2,1,0:T(8,128)} fusion(f32[4,16,64,128]{3,2,1,0:T(8,128)} %get-tuple-element.126, s32[]{:T(128)} %get-tuple-element.125, bf16[24,16,64,128]{3,2,1,0:T(8,128)(2,1)} %bitcast.71, s32[24,16,128]{2,1,0:T(8,128)S(1)} %dynamic-slice_bitcast_fusion.4, bf16[24,16,128]{2,1,0:T(8,128)(2,1)S(1)} %dynamic-slice_bitcast_fusion.5), kind=kOutput, calls=%fused_computation.10.clone.1 | convolution fusion | flops 817889280 | bytes 7111168 | tf_op jit(solution)/shard_map/while/body/eval_jaxpr/kgcs,kgsd->gcd/dot_general | solution.py:27
  125.6 1.8 %fusion.15 = bf16[64,8192]{1,0:T(8,128)(2,1)S(1)} fusion(f32[64,8,8,128]{3,2,1,0:T(8,128)} %bitcast.75, bf16[64,8192]{1,0:T(8,128)(2,1)S(1)} %copy-done.1, f32[]{:T(128)} %bitcast), kind=kLoop, calls=%fused_computation.20 | loop fusion | flops 2097152 | bytes 4194308 | tf_op jit(solution)/shard_map/convert_element_type | solution.py:62
  127.4 0.8 reshape.130
  129.0 35.4 %all_to_all.20 = bf16[64,8,2,512]{3,2,0,1:T(2,128)(2,1)S(1)} all-to-all(bf16[64,8,2,512]{3,2,0,1:T(2,128)(2,1)S(1)} %copy.28), channel_id=1, replica_groups=mesh['dom'=32,'feat'=8] {'feat'}, dimensions={1} | all-to-all | bytes 2097152 | tf_op jit(solution)/shard_map/all_to_all | solution.py:67
  164.6 2.3 %add_convert_fusion = bf16[1024,512]{1,0:T(8,128)(2,1)} fusion(bf16[512,512]{1,0:T(8,128)(2,1)S(1)} %copy-done, bf16[512,1024]{1,0:T(8,128)(2,1)S(1)} %bitcast.76, bf16[512,512]{1,0:T(8,128)(2,1)S(1)} %copy-done.5, f32[512]{0:T(512)S(1)} %copy-done.6, f32[512]{0:T(512)S(1)} %copy-done.7), kind=kOutput, calls=%fused_computation.21 | convolution fusion | flops 1076363264 | bytes 3149824 | tf_op jit(solution)/shard_map/dot_general | solution.py:76
  (50 shorter events, 3.6 us)
Async XLA Ops:
  0.0 164.6 %copy-start = (bf16[512,512]{1,0:T(8,128)(2,1)S(1)}, bf16[512,512]{1,0:T(8,128)(2,1)}, u32[]{:S(2)}) copy-start(bf16[512,512]{1,0:T(8,128)(2,1)} %param.22) | copy-start | bytes 1572868
  10.0 8.8 %copy-start.2 = (s32[24,8192]{1,0:T(8,128)S(1)}, s32[24,8192]{1,0:T(8,128)}, u32[]{:S(2)}) copy-start(s32[24,8192]{1,0:T(8,128)} %param.17) | copy-start | bytes 2359300
  10.0 8.9 %copy-start.4 = (s32[24,64]{1,0:T(8,128)S(1)}, s32[24,64]{1,0:T(8,128)}, u32[]{:S(2)}) copy-start(s32[24,64]{1,0:T(8,128)} %param.16) | copy-start | bytes 18436
  10.0 9.7 %copy-start.3 = (s32[8192]{0:T(1024)S(1)}, s32[8192]{0:T(1024)}, u32[]{:S(2)}) copy-start(s32[8192]{0:T(1024)} %param.18) | copy-start | bytes 98308
  10.0 60.9 %all-to-all-start = ((bf16[32,8,64,128]{3,2,1,0:T(8,128)(2,1)}), bf16[32,8,64,128]{3,2,1,0:T(8,128)(2,1)}, u32[]{:S(2)}, u32[]{:S(2)}) async-start(bf16[32,8,64,128]{3,2,1,0:T(8,128)(2,1)} %broadcast_select_fusion), calls=%async_computation | async-start | bytes 8388608 | tf_op jit(solution)/shard_map/all_to_all | solution.py:55
  75.9 49.6 %copy-start.1 = (bf16[64,8192]{1,0:T(8,128)(2,1)S(1)}, bf16[64,8192]{1,0:T(8,128)(2,1)}, u32[]{:S(2)}) copy-start(bf16[64,8192]{1,0:T(8,128)(2,1)} %param.13) | copy-start | bytes 3145732
  127.4 37.2 %copy-start.5 = (bf16[512,512]{1,0:T(8,128)(2,1)S(1)}, bf16[512,512]{1,0:T(8,128)(2,1)}, u32[]{:S(2)}) copy-start(bf16[512,512]{1,0:T(8,128)(2,1)} %param.20) | copy-start | bytes 1572868
  127.4 37.2 %copy-start.6 = (f32[512]{0:T(512)S(1)}, f32[512]{0:T(512)}, u32[]{:S(2)}) copy-start(f32[512]{0:T(512)} %param.23) | copy-start | bytes 6148
  127.4 37.2 %copy-start.7 = (f32[512]{0:T(512)S(1)}, f32[512]{0:T(512)}, u32[]{:S(2)}) copy-start(f32[512]{0:T(512)} %param.21) | copy-start | bytes 6148
where the time goes:
time: 169 us; the launch traced here: 167 us
  waiting for transfers between devices  50.4 us (30%)
  local copies, waits for them, and re-layouts  37.3 us (22%)
  blocking collectives  35.4 us (21%)
  matrix products  21.3 us (13%)
  other arithmetic  13 us (8%)
  starting transfers between devices  8.77 us (5%)
    all_to_all x1, waiting for transfers between devices, per_device(): lax.all_to_all(chosen, 'dom', split_axis=0, concat_axis=0, tiled=True)  50.4 us
    all_to_all x1, blocking collectives, per_device(): lax.all_to_all(shaped, 'feat', split_axis=1, concat_axis=0, tiled=True)  35.4 us
    gather x4, local copies, waits for them, and re-layouts, one_step(): gathered = table[triple[0]]  26.2 us
    dot_general x4, matrix products, one_step(): jnp.einsum('kgcs,kgsd->gcd', gathered, onehot, preferred_element_type=jnp...  19 us
    all_to_all x1, starting transfers between devices, per_device(): lax.all_to_all(chosen, 'dom', split_axis=0, concat_axis=0, tiled=True)  8.77 us
    concatenate x1, other arithmetic, per_device(): halo_table = jnp.concatenate([feat_blocks, arrived], axis=0)  5.02 us
    select_n x1, other arithmetic, per_device(): jnp.where(slot_used[:, :, None, None], chosen, jnp.zeros_like(chosen))  3.79 us
    broadcast_in_dim x4, local copies, waits for them, and re-layouts, one_step(): jnp.where(triple[1][:, :, None, :] == source_ids, triple[2][:, :, None, :...  3.62 us
  transfers between devices with their start and end apart: 1, of which 1 were waited for; matrix products, arithmetic and copies ran while one was open for 1% of the time, Pallas kernels for 0%

commit v1 on v0

v1 whole, which is shorter than its diff:
```python
import functools

import jax
import jax.numpy as jnp
from jax import lax
from jax.experimental import pallas as pl
from jax.experimental.pallas import tpu as pltpu
from jax.sharding import PartitionSpec as P

MESH = pl.DeviceIdType.MESH
BLOCK = 128
DOM = 32
FEAT = 8
SLOTS = 8
NEIGH = 24
BLOCKS = 64
CHUNKS = 4
WIDTH = 16
UNROLL = 4
OWNED = 1024

OFFSETS = [(a, b, c) for a in range(4) for b in range(4) for c in range(2)][1:]
CLASSES = [[o for o in OFFSETS if o[1] == k] for k in (1, 3, 2, 0)]
ORDER = []
while any(CLASSES):
    for group in CLASSES:
        if group:
            ORDER.append(group.pop(0))


def partner(me, offset):
    x = lax.rem(me // 8 + offset[0], 4)
    y = lax.rem((me // 2) % 4 + offset[1], 4)
    core = lax.rem(me % 2 + offset[2], 2)
    return x * 8 + y * 2 + core


def lane_gather(tile, index):
    return lax.gather(
        tile,
        index[..., None],
        lax.GatherDimensionNumbers(
            offset_dims=(),
            collapsed_slice_dims=(1,),
            start_index_map=(1,),
            operand_batching_dims=(0,),
            start_indices_batching_dims=(0,),
        ),
        slice_sizes=(1, 1),
        mode=lax.GatherScatterMode.PROMISE_IN_BOUNDS,
    )


def kernel(
    send_ref, count_ref, tile_ref, eps_ref, feat_ref, near_ref, degree_ref, w1_ref, b1_ref, w2_ref, b2_ref,
    out_ref, *scratch,
):
    tables, sends, mixes, parcels, owns = (scratch[CHUNKS * k : CHUNKS * (k + 1)] for k in range(5))
    index_ref, pre_ref, dom_send, dom_recv, feat_send, feat_recv = scratch[CHUNKS * 5 :]
    me = lax.axis_index("dom")
    lane = lax.axis_index("feat")

    barrier = pltpu.get_barrier_semaphore()
    for offset in ORDER:
        pl.semaphore_signal(barrier, inc=1, device_id={"dom": partner(me, offset)}, device_id_type=MESH)
    for step in range(1, FEAT):
        pl.semaphore_signal(barrier, inc=1, device_id={"feat": lax.rem(lane + step, FEAT)}, device_id_type=MESH)

    def pack(c):
        def own(b, carry):
            lanes = pl.ds(pl.multiple_of(b * BLOCK, BLOCK), BLOCK)
            block = feat_ref[c * WIDTH : (c + 1) * WIDTH, lanes]
            owns[c][b] = block
            tables[c][b] = block
            return carry

        lax.fori_loop(0, BLOCKS, own, 0, unroll=4)

        def body(p, carry):
            used = jnp.full((WIDTH, BLOCK), count_ref[0, p], jnp.int32)
            for s in range(SLOTS):
                block = owns[c][send_ref[s, p]]
                sends[c][p, s] = jnp.where(s < used, block, jnp.zeros_like(block))
            return carry

        lax.fori_loop(0, DOM, body, 0)

    def launch(c):
        for offset in ORDER:
            p = partner(me, offset)
            pltpu.make_async_remote_copy(
                src_ref=sends[c].at[p],
                dst_ref=tables[c].at[pl.ds(BLOCKS + me * SLOTS, SLOTS)],
                send_sem=dom_send.at[c],
                recv_sem=dom_recv.at[c],
                device_id={"dom": p},
                device_id_type=MESH,
            ).start()

    for c in range(CHUNKS):
        pack(c)
        if c == 0:
            pl.semaphore_wait(barrier, DOM + FEAT - 2)
        launch(c)

    def stage(b, carry):
        lanes = pl.ds(pl.multiple_of(b * BLOCK, BLOCK), BLOCK)
        for j in range(NEIGH):
            index_ref[b, j] = jnp.broadcast_to(near_ref[j : j + 1, lanes], (WIDTH, BLOCK)).astype(jnp.int16)
        return carry

    lax.fori_loop(0, BLOCKS, stage, 0)
    for c in range(CHUNKS):
        for s in range(SLOTS):
            tables[c][BLOCKS + me * SLOTS + s] = jnp.zeros((WIDTH, BLOCK), jnp.bfloat16)

    weight = 1.0 + eps_ref[0]

    def to_feat(c, g):
        return pltpu.make_async_remote_copy(
            src_ref=mixes[c].at[g],
            dst_ref=parcels[c].at[lane],
            send_sem=feat_send.at[c],
            recv_sem=feat_recv.at[c],
            device_id={"feat": g},
            device_id_type=MESH,
        )

    def aggregate(c):
        table = tables[c]

        def group(i, carry):
            g = lax.rem(lane + 1 + i, FEAT)

            def part(h, inner):
                for u in range(UNROLL):
                    at = h * UNROLL + u
                    b = g * 8 + at
                    limit = jnp.broadcast_to(
                        degree_ref[:, pl.ds(pl.multiple_of(b * BLOCK, BLOCK), BLOCK)], (8, BLOCK)
                    )
                    own = owns[c][b].astype(jnp.float32)
                    low, high = weight * own[:8], weight * own[8:]
                    for j in range(NEIGH):
                        got = lane_gather(table[tile_ref[j, b]], index_ref[b, j]).astype(jnp.float32)
                        live = j < limit
                        low = low + jnp.where(live, got[:8], 0.0)
                        high = high + jnp.where(live, got[8:], 0.0)
                    mixes[c][g, :, pl.ds(pl.multiple_of(at * BLOCK, BLOCK), BLOCK)] = jnp.concatenate(
                        [low, high], 0
                    ).astype(jnp.bfloat16)
                return inner

            lax.fori_loop(0, 8 // UNROLL, part, 0)

            @pl.when(i < FEAT - 1)
            def _():
                to_feat(c, g).start()

            return carry

        lax.fori_loop(0, FEAT, group, 0)
        parcels[c][lane] = mixes[c][lane]

    def mlp(c):
        held = parcels[c].at[pl.ds(0, FEAT - 1)]
        pltpu.make_async_copy(held, held, feat_recv.at[c]).wait()
        w1 = jnp.concatenate([w1_ref[f * 64 + c * WIDTH : f * 64 + (c + 1) * WIDTH] for f in range(FEAT)], 0)

        def body(r, carry):
            rows = pl.ds(pl.multiple_of(r * 256, 256), 256)
            cols = parcels[c][:, :, rows].reshape(FEAT * WIDTH, 256)
            part = lax.dot_general(cols, w1, (((0,), (0,)), ((), ())), preferred_element_type=jnp.float32)
            if c == 0:
                pre_ref[rows] = part + b1_ref[...]
            elif c < CHUNKS - 1:
                pre_ref[rows] += part
            else:
                act = jnp.maximum(pre_ref[rows] + part, 0.0).astype(jnp.bfloat16)
                out_ref[rows] = (
                    jnp.dot(act, w2_ref[...], preferred_element_type=jnp.float32) + b2_ref[...]
                ).astype(jnp.bfloat16)
            return carry

        lax.fori_loop(0, OWNED // 256, body, 0)

    for c in range(CHUNKS):
        landed = tables[c].at[pl.ds(BLOCKS, (DOM - 1) * SLOTS)]
        pltpu.make_async_copy(landed, landed, dom_recv.at[c]).wait()
        aggregate(c)
        if c > 0:
            mlp(c - 1)
    mlp(CHUNKS - 1)
    for c in range(CHUNKS):
        sent = sends[c].at[pl.ds(0, DOM - 1)]
        pltpu.make_async_copy(sent, sent, dom_send.at[c]).wait()
        left = mixes[c].at[pl.ds(0, FEAT - 1)]
        pltpu.make_async_copy(left, left, feat_send.at[c]).wait()


def per_device(
    features, send_blocks, counts, tile_blocks, neighbours, degree, epsilon, w_first, b_first, w_second, b_second
):
    smem = pl.BlockSpec(memory_space=pltpu.SMEM)
    vmem = pl.BlockSpec(memory_space=pltpu.VMEM)
    bf16 = jnp.bfloat16
    return pl.pallas_call(
        kernel,
        out_shape=jax.ShapeDtypeStruct((OWNED, w_second.shape[1]), bf16),
        in_specs=[smem] * 4 + [vmem] * 7,
        out_specs=vmem,
        scratch_shapes=[pltpu.VMEM((BLOCKS + DOM * SLOTS, WIDTH, BLOCK), bf16)] * CHUNKS
        + [pltpu.VMEM((DOM, SLOTS, WIDTH, BLOCK), bf16)] * CHUNKS
        + [pltpu.VMEM((FEAT, WIDTH, OWNED), bf16)] * CHUNKS
        + [pltpu.VMEM((FEAT, WIDTH, OWNED), bf16)] * CHUNKS
        + [pltpu.VMEM((BLOCKS, WIDTH, BLOCK), bf16)] * CHUNKS
        + [
            pltpu.VMEM((BLOCKS, NEIGH, WIDTH, BLOCK), jnp.int16),
            pltpu.VMEM((OWNED, w_first.shape[1]), jnp.float32),
        ]
        + [pltpu.SemaphoreType.DMA((CHUNKS,))] * 4,
        compiler_params=pltpu.CompilerParams(
            collective_id=0, has_side_effects=True, vmem_limit_bytes=52 * 1024 * 1024
        ),
        name="gin",
    )(
        send_blocks[0].T,
        counts,
        tile_blocks,
        epsilon,
        features,
        neighbours,
        degree[None],
        w_first,
        b_first[None],
        w_second,
        b_second[None],
    )


def solution(mesh):
    return jax.shard_map(
        per_device,
        mesh=mesh,
        in_specs=(
            P("feat", "dom"),
            P("dom", None, None),
            P("dom", None),
            P(None, "dom"),
            P(None, "dom"),
            P("dom"),
            P(),
            P(),
            P(),
            P(),
            P(),
        ),
        out_specs=P(("dom", "feat"), None),
        check_vma=False,
    )
```

time: 169 us -> 83.1 us (0.49)
  Pallas kernels: 0 us -> 74.3 us
  waiting for transfers between devices: 50.4 us -> 0 us
  blocking collectives: 35.4 us -> 0 us
  local copies, waits for them, and re-layouts: 37.3 us -> 7.61 us
  matrix products: 21.3 us -> 0 us
  other arithmetic: 13 us -> 0 us
  starting transfers between devices: 8.77 us -> 0 us
    pallas_call x0 -> x1, Pallas kernels: none -> 74.3 us  [per_device(): pl.pallas_call(kernel, out_shape=jax.ShapeDtypeStruct((OWNED, w_second.sh...]
    all_to_all x1 -> x0, waiting for transfers between devices: 50.4 us -> none  [per_device(): lax.all_to_all(chosen, 'dom', split_axis=0, concat_axis=0, tiled=True)]
    all_to_all x1 -> x0, blocking collectives: 35.4 us -> none  [per_device(): lax.all_to_all(shaped, 'feat', split_axis=1, concat_axis=0, tiled=True)]
    gather x5 -> x0, local copies, waits for them, and re-layouts: 29.2 us -> none  [the longest x4 26.2 us: one_step(): gathered = table[triple[0]]]
    dot_general x5 -> x0, matrix products: 21.3 us -> none  [the longest x4 19 us: one_step(): jnp.einsum('kgcs,kgsd->gcd', gathered, onehot, preferred_element_type=jnp...]
    all_to_all x1 -> x0, starting transfers between devices: 8.77 us -> none  [per_device(): lax.all_to_all(chosen, 'dom', split_axis=0, concat_axis=0, tiled=True)]
    unnamed x19, local copies, waits for them, and re-layouts: 0.5 us -> 7.61 us
    concatenate x1 -> x0, other arithmetic: 5.02 us -> none  [per_device(): halo_table = jnp.concatenate([feat_blocks, arrived], axis=0)]
  transfers between devices with their start and end apart: 1 -> 0, of which waited for: 1 -> 0; matrix products, arithmetic and copies ran while one was open for 1% -> 0% of each run, Pallas kernels for 0% -> 0%
where the time goes in v1:
time: 83.1 us; the launch traced here: 82.7 us
  Pallas kernels  74.3 us (89%)
  local copies, waits for them, and re-layouts  7.61 us (9%)
    pallas_call x1, Pallas kernels, per_device(): pl.pallas_call(kernel, out_shape=jax.ShapeDtypeStruct((OWNED, w_second.sh...  74.3 us
    unnamed x19, local copies, waits for them, and re-layouts  7.61 us

profile of v1, /device:TPU:1, one launch (start us, length us, event | category | flops | bytes accessed | tf_op | source)
XLA Modules:
  0.0 82.7 jit_solution(9363673150690857063)
XLA Ops:
  0.0 0.0 copy-start.7
  0.7 0.0 copy-start.5
  0.7 0.0 copy-start.6
  0.7 0.0 copy-start.8
  0.7 0.0 copy-done.7
  0.7 0.6 copy-done.5
  1.4 0.0 copy-done.6
  1.4 0.0 copy-done.8
  1.4 0.0 copy-start
  1.4 1.1 %copy-done = s32[24,8192]{1,0:T(8,128)S(1)} copy-done((s32[24,8192]{1,0:T(8,128)S(1)}, s32[24,8192]{1,0:T(8,128)}, u32[]{:S(2)}) %copy-start) | copy-done | bytes 786456
  2.5 0.0 copy-start.1
  2.5 1.0 %copy-done.1 = bf16[512,512]{1,0:T(8,128)(2,1)S(1)} copy-done((bf16[512,512]{1,0:T(8,128)(2,1)S(1)}, bf16[512,512]{1,0:T(8,128)(2,1)}, u32[]{:S(2)}) %copy-start.1) | copy-done | bytes 524312
  3.5 0.0 copy-start.2
  3.5 1.0 %copy-done.2 = bf16[512,512]{1,0:T(8,128)(2,1)S(1)} copy-done((bf16[512,512]{1,0:T(8,128)(2,1)S(1)}, bf16[512,512]{1,0:T(8,128)(2,1)}, u32[]{:S(2)}) %copy-start.2) | copy-done | bytes 524312
  4.6 0.0 copy-start.3
  4.6 0.8 copy-done.3
  5.3 0.0 copy-start.4
  5.3 0.7 copy-done.4
  6.1 74.3 %gin.1 = bf16[1024,512]{1,0:T(8,128)(2,1)} custom-call(s32[8,32]{1,0:T(8,128)S(1)} %bitcast.7, s32[1,32]{1,0:T(1,128)S(1)} %copy-done.8, s32[24,64]{1,0:T(8,128)S(1)} %copy-done.4, f32[1]{0:T(128)S(6)} %copy.13.eps_ref, bf16[64,8192]{1,0:T(8,128)(2,1)} %feat_ref.1, s32[24,8192]{1,0:T(8,128)S(1)} %copy-done, s32[1,8192]{1,0:T(1,128)S(1)} %bitcast.6, ...), custom_call_target="tpu_custom_call" | custom-call | tf_op jit(solution)/shard_map/gin/pallas_call | solution.py:207
  80.4 2.3 %copy.14 = bf16[1024,512]{1,0:T(8,128)(2,1)} copy(bf16[1024,512]{1,0:T(8,128)(2,1)} %gin.1) | data formatting | bytes 2097152
Async XLA Ops:
  0.0 0.7 copy-start.7
  0.7 0.7 copy-start.5
  0.7 0.7 copy-start.6
  0.7 0.7 copy-start.8
  1.4 1.1 %copy-start = (s32[24,8192]{1,0:T(8,128)S(1)}, s32[24,8192]{1,0:T(8,128)}, u32[]{:S(2)}) copy-start(s32[24,8192]{1,0:T(8,128)} %near_ref.1) | copy-start | bytes 2359300
  2.5 1.0 %copy-start.1 = (bf16[512,512]{1,0:T(8,128)(2,1)S(1)}, bf16[512,512]{1,0:T(8,128)(2,1)}, u32[]{:S(2)}) copy-start(bf16[512,512]{1,0:T(8,128)(2,1)} %w1_ref.1) | copy-start | bytes 1572868
  3.5 1.0 %copy-start.2 = (bf16[512,512]{1,0:T(8,128)(2,1)S(1)}, bf16[512,512]{1,0:T(8,128)(2,1)}, u32[]{:S(2)}) copy-start(bf16[512,512]{1,0:T(8,128)(2,1)} %w2_ref.1) | copy-start | bytes 1572868
  4.6 0.8 copy-start.3
  5.3 0.7 copy-start.4

commit v2 on v1

v2 whole, which is shorter than its diff:
```python
import functools

import jax
import jax.numpy as jnp
from jax import lax
from jax.experimental import pallas as pl
from jax.experimental.pallas import tpu as pltpu
from jax.sharding import PartitionSpec as P

MESH = pl.DeviceIdType.MESH
BLOCK = 128
DOM = 32
FEAT = 8
SLOTS = 8
NEIGH = 24
BLOCKS = 64
CHUNKS = 4
WIDTH = 16
UNROLL = 8
OWNED = 1024

RING = 4
PLAN = ("s0", "s1", "t0", "f0", "n0", "d0", "f1", "n1", "r0", "d1", "r1", "d2", "d3", "a0", "d4", "d5", "d6", "d7", "a1", "m0", "a2", "m1", "a3", "m2", "m3")
RINGS = 2
HALF = BLOCKS // 2
WAVE = [(1, 0), (3, 0), (2, 0), (1, 1), (3, 1), (2, 1), (0, 1)]


OFFSETS = [(a, b, c) for a in range(4) for b in range(4) for c in range(2)][1:]
CLASSES = [[o for o in OFFSETS if o[1] == k] for k in (1, 3, 2, 0)]
ORDER = []
while any(CLASSES):
    for group in CLASSES:
        if group:
            ORDER.append(group.pop(0))
PARTS = 4


def lane_gather(tile, index):
    return lax.gather(
        tile,
        index[..., None],
        lax.GatherDimensionNumbers(
            offset_dims=(),
            collapsed_slice_dims=(1,),
            start_index_map=(1,),
            operand_batching_dims=(0,),
            start_indices_batching_dims=(0,),
        ),
        slice_sizes=(1, 1),
        mode=lax.GatherScatterMode.PROMISE_IN_BOUNDS,
    )


def kernel(
    send_hbm, count_hbm, tile_hbm, eps_ref, feat_hbm, near_hbm, degree_hbm, w1_hbm, b1_hbm,
    out_ref, *scratch,
):
    tables, sends, mixes, parcels, owns, rights, fars, lefts = (
        scratch[CHUNKS * k : CHUNKS * (k + 1)] for k in range(8)
    )
    (*index_v, index_0, index_1, index_2, index_3) = scratch[CHUNKS * 8 : CHUNKS * 8 + 2 * RING]
    picks = (index_0, index_1, index_2, index_3)
    (
        send_ref, count_ref, tile_ref, feat_ref, near_ref, degree_ref, w1_ref, b1_ref,
        index_ref, flat_ref, pre_ref, dom_send, dom_recv, feat_send, feat_recv, load_sem,
        ring_send, ring_recv, pick_send, pick_recv, pick_load,
    ) = scratch[CHUNKS * 8 + 2 * RING :]
    loads = [
        pltpu.make_async_copy(src, dst, load_sem.at[i])
        for i, (src, dst) in enumerate(
            (
                (feat_hbm, feat_ref),
                (send_hbm, send_ref),
                (count_hbm, count_ref),
                (tile_hbm, tile_ref),
                (near_hbm, near_ref),
                (degree_hbm, degree_ref),
                (w1_hbm, w1_ref),
                (b1_hbm, b1_ref),
            )
        )
    ]
    for load in loads:
        load.start()
    me = lax.axis_index("dom")
    lane = lax.axis_index("feat")
    x, y, core = me // 8, (me // 2) % RING, me % 2
    first_at, second_at = x + (y - x) * core, y + (x - y) * core
    first_step, second_step = 8 - 6 * core, 2 + 6 * core

    def along(r):
        return me + (lax.rem(first_at + r, RING) - first_at) * first_step

    def across(t, flip):
        return me + (lax.rem(second_at + t, RING) - second_at) * second_step + flip * (1 - 2 * core)

    barrier = pltpu.get_barrier_semaphore()
    for dx, dy, flip in ORDER:
        p = lax.rem(x + dx, RING) * 8 + lax.rem(y + dy, RING) * 2 + lax.rem(core + flip, 2)
        pl.semaphore_signal(barrier, inc=1, device_id={"dom": p}, device_id_type=MESH)
    for step in range(1, FEAT):
        pl.semaphore_signal(barrier, inc=1, device_id={"feat": lax.rem(lane + step, FEAT)}, device_id_type=MESH)

    def ring(c, src, dst, part, k, r):
        pltpu.make_async_remote_copy(
            src_ref=src[c].at[pl.ds(part * HALF, HALF)],
            dst_ref=dst[c].at[pl.ds(part * HALF, HALF)],
            send_sem=ring_send.at[c],
            recv_sem=ring_recv.at[c, k],
            device_id={"dom": along(r)},
            device_id_type=MESH,
        ).start()

    def ring_wait(c, k):
        half = owns[c].at[pl.ds(0, HALF)]
        pltpu.make_async_copy(half, half, ring_recv.at[c, k]).wait()

    def own(c):
        def body(b, carry):
            lanes = pl.ds(pl.multiple_of(b * BLOCK, BLOCK), BLOCK)
            block = feat_ref[c * WIDTH : (c + 1) * WIDTH, lanes]
            owns[c][b] = block
            tables[c][b] = block
            return carry

        lax.fori_loop(0, BLOCKS, body, 0, unroll=4)
        for buffers in (owns, rights, fars, lefts):
            buffers[c][BLOCKS] = jnp.zeros((WIDTH, BLOCK), jnp.bfloat16)

    def wave(c, r):
        source = (owns, rights, fars, lefts)[r][c]
        q = along(r)
        if r > 0:
            for s in range(SLOTS):
                tables[c][BLOCKS + q * SLOTS + s] = source[picks[r][s, me]]
        else:
            for s in range(SLOTS):
                tables[c][BLOCKS + q * SLOTS + s] = jnp.zeros((WIDTH, BLOCK), jnp.bfloat16)
        for k, (t, flip) in enumerate(WAVE):
            p = across(t, flip)
            for s in range(SLOTS):
                sends[c][r * len(WAVE) + k, s] = source[picks[r][s, p]]
        for k, (t, flip) in enumerate(WAVE):
            pltpu.make_async_remote_copy(
                src_ref=sends[c].at[r * len(WAVE) + k],
                dst_ref=tables[c].at[pl.ds(BLOCKS + q * SLOTS, SLOTS)],
                send_sem=dom_send.at[c],
                recv_sem=dom_recv.at[c],
                device_id={"dom": across(t, flip)},
                device_id_type=MESH,
            ).start()

    def forward(c):
        ring_wait(c, 0)
        ring(c, lefts, fars, 0, 4, 1)
        ring_wait(c, 2)
        ring(c, rights, fars, 1, 5, 3)

    def near(c):
        ring_wait(c, 1)
        wave(c, 3)
        ring_wait(c, 3)
        wave(c, 1)

    def far(c):
        ring_wait(c, 4)
        ring_wait(c, 5)
        wave(c, 2)

    for load in loads[:3]:
        load.wait()
    slot = lax.broadcasted_iota(jnp.int32, (SLOTS, DOM), 0)
    index_v[0][...] = jnp.where(slot < count_ref[...], send_ref[...], BLOCKS)
    own_pick = pltpu.make_async_copy(index_v[0], picks[0], pick_load.at[0])
    own_pick.start()
    def hand(r):
        return pltpu.make_async_remote_copy(
            src_ref=index_v[0],
            dst_ref=index_v[r],
            send_sem=pick_send.at[r],
            recv_sem=pick_recv.at[r],
            device_id={"dom": along(RING - r)},
            device_id_type=MESH,
        )

    def direct(c, part):
        if part == 0:
            own(c)
            for s in range(SLOTS):
                tables[c][BLOCKS + me * SLOTS + s] = jnp.zeros((WIDTH, BLOCK), jnp.bfloat16)
        group = list(enumerate(ORDER))[part * len(ORDER) // PARTS : (part + 1) * len(ORDER) // PARTS]

        def peer(offset):
            return (
                lax.rem(x + offset[0], RING) * 8
                + lax.rem(y + offset[1], RING) * 2
                + lax.rem(core + offset[2], 2)
            )

        for k, offset in group:
            p = peer(offset)
            for s in range(SLOTS):
                sends[c][k, s] = owns[c][picks[0][s, p]]
        for k, offset in group:
            pltpu.make_async_remote_copy(
                src_ref=sends[c].at[k],
                dst_ref=tables[c].at[pl.ds(BLOCKS + me * SLOTS, SLOTS)],
                send_sem=dom_send.at[c],
                recv_sem=dom_recv.at[c],
                device_id={"dom": peer(offset)},
                device_id_type=MESH,
            ).start()

    def start(c):
        own(c)
        if c == 0:
            pl.semaphore_wait(barrier, DOM + FEAT - 2)
        ring(c, owns, lefts, 0, 0, 1)
        ring(c, owns, rights, 1, 2, 3)
        ring(c, owns, lefts, 1, 1, 1)
        ring(c, owns, rights, 0, 3, 3)
        if c == 0:
            own_pick.wait()
            for r in range(1, RING):
                hand(r).start()
        wave(c, 0)

    def stage():
        for load in loads[3:]:
            load.wait()

        def body(b, carry):
            lanes = pl.ds(pl.multiple_of(b * BLOCK, BLOCK), BLOCK)
            for j in range(NEIGH):
                flat_ref[b * NEIGH + j] = tile_ref[j, b]
            for j in range(NEIGH):
                index_ref[b, j] = jnp.broadcast_to(near_ref[j : j + 1, lanes], (WIDTH, BLOCK)).astype(jnp.int16)
            return carry

        lax.fori_loop(0, BLOCKS, body, 0)
        for r in range(1, RING):
            hand(r).wait()
        loaded = [pltpu.make_async_copy(index_v[r], picks[r], pick_load.at[r]) for r in range(1, RING)]
        for load in loaded:
            load.start()
        for load in loaded:
            load.wait()

    weight = 1.0 + eps_ref[0]

    def to_feat(c, g):
        return pltpu.make_async_remote_copy(
            src_ref=mixes[c].at[g],
            dst_ref=parcels[c].at[lane],
            send_sem=feat_send.at[c],
            recv_sem=feat_recv.at[c],
            device_id={"feat": g},
            device_id_type=MESH,
        )

    def aggregate(c, first, last):
        table = tables[c]

        def group(i, carry):
            g = lax.rem(lane + 1 + i, FEAT)

            def part(h, inner):
                for u in range(UNROLL):
                    at = h * UNROLL + u
                    b = g * 8 + at
                    limit = jnp.broadcast_to(
                        degree_ref[:, pl.ds(pl.multiple_of(b * BLOCK, BLOCK), BLOCK)], (8, BLOCK)
                    )
                    own = owns[c][b].astype(jnp.float32)
                    low, high = weight * own[:8], weight * own[8:]
                    for j in range(NEIGH):
                        got = lane_gather(table[flat_ref[b * NEIGH + j]], index_ref[b, j]).astype(jnp.float32)
                        live = j < limit
                        low = low + jnp.where(live, got[:8], 0.0)
                        high = high + jnp.where(live, got[8:], 0.0)
                    mixes[c][g, :, pl.ds(pl.multiple_of(at * BLOCK, BLOCK), BLOCK)] = jnp.concatenate(
                        [low, high], 0
                    ).astype(jnp.bfloat16)
                return inner

            lax.fori_loop(0, 8 // UNROLL, part, 0)

            @pl.when(i < FEAT - 1)
            def _():
                to_feat(c, g).start()

            return carry

        if first == 0:
            landed = tables[c].at[pl.ds(BLOCKS, (RING * len(WAVE) if c < RINGS else len(ORDER)) * SLOTS)]
            pltpu.make_async_copy(landed, landed, dom_recv.at[c]).wait()
        lax.fori_loop(first, last, group, 0)
        if last == FEAT:
            parcels[c][lane] = mixes[c][lane]

    def mlp(c, first, last):
        held = parcels[c].at[pl.ds(0, FEAT - 1)]
        pltpu.make_async_copy(held, held, feat_recv.at[c]).wait()
        w1 = jnp.concatenate([w1_ref[f * 64 + c * WIDTH : f * 64 + (c + 1) * WIDTH] for f in range(FEAT)], 0)

        def body(r, carry):
            rows = pl.ds(pl.multiple_of(r * 256, 256), 256)
            cols = parcels[c][:, :, rows].reshape(FEAT * WIDTH, 256)
            part = lax.dot_general(cols, w1, (((0,), (0,)), ((), ())), preferred_element_type=jnp.float32)
            if first:
                pre_ref[rows] = part + b1_ref[...]
            elif not last:
                pre_ref[rows] += part
            else:
                out_ref[rows] = jnp.maximum(pre_ref[rows] + part, 0.0).astype(jnp.bfloat16)
            return carry

        lax.fori_loop(0, OWNED // 256, body, 0)

    merges = [int(step[1]) for step in PLAN if step[0] == "m"]
    for step in PLAN:
        op, c = step[0], ord(step[1]) - 48
        if op == "s":
            start(c)
        elif op == "d":
            direct(RINGS + c // PARTS, c % PARTS)
        elif op == "t":
            stage()
        elif op == "f":
            forward(c)
        elif op == "n":
            near(c)
        elif op == "r":
            far(c)
        elif op == "a":
            aggregate(c, 0, FEAT)
        elif op == "b":
            aggregate(c, 0, FEAT // 2)
        elif op == "e":
            aggregate(c, FEAT // 2, FEAT)
        elif op == "m":
            mlp(c, c == merges[0], c == merges[-1])
    for c in range(CHUNKS):
        pltpu.make_async_copy(sends[c], sends[c], dom_send.at[c]).wait()
        if c < RINGS:
            ringed = tables[c].at[pl.ds(0, 6 * HALF)]
            pltpu.make_async_copy(ringed, ringed, ring_send.at[c]).wait()
        left = mixes[c].at[pl.ds(0, FEAT - 1)]
        pltpu.make_async_copy(left, left, feat_send.at[c]).wait()


def per_device(
    features, send_blocks, counts, tile_blocks, neighbours, degree, epsilon, w_first, b_first, w_second, b_second
):
    smem = pl.BlockSpec(memory_space=pltpu.SMEM)
    vmem = pl.BlockSpec(memory_space=pltpu.VMEM)
    hbm = pl.BlockSpec(memory_space=pl.ANY)
    bf16 = jnp.bfloat16
    int32 = jnp.int32
    hidden = w_first.shape[1]
    activated = pl.pallas_call(
        kernel,
        out_shape=jax.ShapeDtypeStruct((OWNED, hidden), bf16),
        in_specs=[hbm] * 3 + [smem] + [hbm] * 5,
        out_specs=vmem,
        scratch_shapes=[pltpu.VMEM((BLOCKS + DOM * SLOTS, WIDTH, BLOCK), bf16)] * CHUNKS
        + [
            pltpu.VMEM((RING * len(WAVE) if c < RINGS else len(ORDER), SLOTS, WIDTH, BLOCK), bf16)
            for c in range(CHUNKS)
        ]
        + [pltpu.VMEM((FEAT, WIDTH, OWNED), bf16)] * CHUNKS
        + [pltpu.VMEM((FEAT, WIDTH, OWNED), bf16)] * CHUNKS
        + [pltpu.VMEM((BLOCKS + 1, WIDTH, BLOCK), bf16)] * (4 * CHUNKS)
        + [pltpu.VMEM((SLOTS, DOM), int32)] * RING
        + [pltpu.SMEM((SLOTS, DOM), int32)] * RING
        + [
            pltpu.VMEM((SLOTS, DOM), int32),
            pltpu.VMEM((1, DOM), int32),
            pltpu.SMEM((NEIGH, BLOCKS), int32),
            pltpu.VMEM(features.shape, bf16),
            pltpu.VMEM(neighbours.shape, int32),
            pltpu.VMEM((1, degree.shape[0]), int32),
            pltpu.VMEM(w_first.shape, bf16),
            pltpu.VMEM((1, hidden), jnp.float32),
            pltpu.VMEM((BLOCKS, NEIGH, WIDTH, BLOCK), jnp.int16),
            pltpu.SMEM((BLOCKS * NEIGH,), int32),
            pltpu.VMEM((OWNED, hidden), jnp.float32),
        ]
        + [pltpu.SemaphoreType.DMA((CHUNKS,))] * 4
        + [pltpu.SemaphoreType.DMA((8,))]
        + [pltpu.SemaphoreType.DMA((RINGS,)), pltpu.SemaphoreType.DMA((RINGS, 6))]
        + [pltpu.SemaphoreType.DMA((RING,))] * 3,
        compiler_params=pltpu.CompilerParams(
            collective_id=0, has_side_effects=True, vmem_limit_bytes=60 * 1024 * 1024
        ),
        name="gin",
    )(send_blocks[0].T, counts, tile_blocks, epsilon, features, neighbours, degree[None], w_first, b_first[None])
    return (jnp.dot(activated, w_second, preferred_element_type=jnp.float32) + b_second).astype(bf16)


def solution(mesh):
    return jax.shard_map(
        per_device,
        mesh=mesh,
        in_specs=(
            P("feat", "dom"),
            P("dom", None, None),
            P("dom", None),
            P(None, "dom"),
            P(None, "dom"),
            P("dom"),
            P(),
            P(),
            P(),
            P(),
            P(),
        ),
        out_specs=P(("dom", "feat"), None),
        check_vma=False,
    )
```

time: 83.1 us -> 73.8 us (0.89)
  local copies, waits for them, and re-layouts: 7.61 us -> 0.01 us
  Pallas kernels: 74.3 us -> 69.1 us
  matrix products: 0 us -> 2.9 us
    unnamed x19 -> x4, local copies, waits for them, and re-layouts: 7.61 us -> 0.01 us
    pallas_call x1, Pallas kernels: 74.3 us -> 69.1 us  [per_device(): pl.pallas_call(kernel, out_shape=jax.ShapeDtypeStruct((OWNED, hidden), bf...]
    dot_general x0 -> x1, matrix products: none -> 2.9 us  [per_device(): jnp.dot(activated, w_second, preferred_element_type=jnp.float32) + b_second]
where the time goes in v2:
time: 73.8 us; the launch traced here: 72.8 us
  Pallas kernels  69.1 us (94%)
  matrix products  2.9 us (4%)
  between operations  0.74 us (1%)
    pallas_call x1, Pallas kernels, per_device(): pl.pallas_call(kernel, out_shape=jax.ShapeDtypeStruct((OWNED, hidden), bf...  69.1 us
    dot_general x1, matrix products, per_device(): jnp.dot(activated, w_second, preferred_element_type=jnp.float32) + b_second  2.9 us

profile of v2, /device:TPU:1, one launch (start us, length us, event | category | flops | bytes accessed | tf_op | source)
XLA Modules:
  0.0 72.8 jit_solution(10207790125909774832)
XLA Ops:
  0.0 0.0 copy-start
  0.7 0.0 copy-start.1
  0.7 69.1 %gin.1 = bf16[1024,512]{1,0:T(8,128)(2,1)} custom-call(s32[8,32]{1,0:T(8,128)} %bitcast.8, s32[1,32]{1,0:T(1,128)} %count_hbm.1, s32[24,64]{1,0:T(8,128)} %tile_hbm.1, f32[1]{0:T(128)S(6)} %copy.12.eps_ref, bf16[64,8192]{1,0:T(8,128)(2,1)} %feat_hbm.1, s32[24,8192]{1,0:T(8,128)} %near_hbm.1, s32[1,8192]{1,0:T(1,128)} %bitcast.7, bf16[512,512]{1,0:T(8,128)(2,1)} %w1_hbm.1, ...), custom_call_target="tpu_custom_call" | custom-call | tf_op jit(solution)/shard_map/gin/pallas_call | solution.py:362
  69.9 0.0 copy-done
  69.9 0.0 copy-done.1
  69.9 2.9 %add_convert_fusion = bf16[1024,512]{1,0:T(8,128)(2,1)} fusion(bf16[1024,512]{1,0:T(8,128)(2,1)} %gin.1, bf16[512,512]{1,0:T(8,128)(2,1)S(1)} %copy-done, f32[512]{0:T(512)S(1)} %copy-done.1), kind=kOutput, calls=%fused_computation | convolution fusion | flops 537919488 | bytes 2623488 | tf_op jit(solution)/shard_map/dot_general | solution.py:399
Async XLA Ops:
  0.0 69.9 %copy-start = (bf16[512,512]{1,0:T(8,128)(2,1)S(1)}, bf16[512,512]{1,0:T(8,128)(2,1)}, u32[]{:S(2)}) copy-start(bf16[512,512]{1,0:T(8,128)(2,1)} %param.20) | copy-start | bytes 1572868
  0.7 69.2 %copy-start.1 = (f32[512]{0:T(512)S(1)}, f32[512]{0:T(512)}, u32[]{:S(2)}) copy-start(f32[512]{0:T(512)} %param.21) | copy-start | bytes 6148

commit v3 on v2

--- a/solution.py
+++ b/solution.py
@@ -20,7 +20,7 @@
 OWNED = 1024
 
 RING = 4
-PLAN = ("s0", "s1", "t0", "f0", "n0", "d0", "f1", "n1", "r0", "d1", "r1", "d2", "d3", "a0", "d4", "d5", "d6", "d7", "a1", "m0", "a2", "m1", "a3", "m2", "m3")
+PLAN = ("s0", "s1", "t0", "f0", "n0", "d0", "f1", "n1", "r0", "d1", "r1", "d2", "d3", "b0", "d4", "d5", "e0", "d6", "d7", "a1", "m0", "a2", "m1", "a3", "m2", "m3")
 RINGS = 2
 HALF = BLOCKS // 2
 WAVE = [(1, 0), (3, 0), (2, 0), (1, 1), (3, 1), (2, 1), (0, 1)]
@@ -64,7 +64,7 @@
     (
         send_ref, count_ref, tile_ref, feat_ref, near_ref, degree_ref, w1_ref, b1_ref,
         index_ref, flat_ref, pre_ref, dom_send, dom_recv, feat_send, feat_recv, load_sem,
-        ring_send, ring_recv, pick_send, pick_recv, pick_load,
+        ring_send, ring_recv, pick_send, pick_recv, pick_load, act_ref, out_sem,
     ) = scratch[CHUNKS * 8 + 2 * RING :]
     loads = [
         pltpu.make_async_copy(src, dst, load_sem.at[i])
@@ -313,7 +313,8 @@
             elif not last:
                 pre_ref[rows] += part
             else:
-                out_ref[rows] = jnp.maximum(pre_ref[rows] + part, 0.0).astype(jnp.bfloat16)
+                act_ref[rows] = jnp.maximum(pre_ref[rows] + part, 0.0).astype(jnp.bfloat16)
+                pltpu.make_async_copy(act_ref.at[rows], out_ref.at[rows], out_sem).start()
             return carry
 
         lax.fori_loop(0, OWNED // 256, body, 0)
@@ -348,13 +349,13 @@
             pltpu.make_async_copy(ringed, ringed, ring_send.at[c]).wait()
         left = mixes[c].at[pl.ds(0, FEAT - 1)]
         pltpu.make_async_copy(left, left, feat_send.at[c]).wait()
+    pltpu.make_async_copy(act_ref, out_ref, out_sem).wait()
 
 
 def per_device(
     features, send_blocks, counts, tile_blocks, neighbours, degree, epsilon, w_first, b_first, w_second, b_second
 ):
     smem = pl.BlockSpec(memory_space=pltpu.SMEM)
-    vmem = pl.BlockSpec(memory_space=pltpu.VMEM)
     hbm = pl.BlockSpec(memory_space=pl.ANY)
     bf16 = jnp.bfloat16
     int32 = jnp.int32
@@ -363,7 +364,7 @@
         kernel,
         out_shape=jax.ShapeDtypeStruct((OWNED, hidden), bf16),
         in_specs=[hbm] * 3 + [smem] + [hbm] * 5,
-        out_specs=vmem,
+        out_specs=hbm,
         scratch_shapes=[pltpu.VMEM((BLOCKS + DOM * SLOTS, WIDTH, BLOCK), bf16)] * CHUNKS
         + [
             pltpu.VMEM((RING * len(WAVE) if c < RINGS else len(ORDER), SLOTS, WIDTH, BLOCK), bf16)
@@ -390,7 +391,8 @@
         + [pltpu.SemaphoreType.DMA((CHUNKS,))] * 4
         + [pltpu.SemaphoreType.DMA((8,))]
         + [pltpu.SemaphoreType.DMA((RINGS,)), pltpu.SemaphoreType.DMA((RINGS, 6))]
-        + [pltpu.SemaphoreType.DMA((RING,))] * 3,
+        + [pltpu.SemaphoreType.DMA((RING,))] * 3
+        + [pltpu.VMEM((OWNED, hidden), bf16), pltpu.SemaphoreType.DMA],
         compiler_params=pltpu.CompilerParams(
             collective_id=0, has_side_effects=True, vmem_limit_bytes=60 * 1024 * 1024
         ),

time: 73.8 us -> 72.8 us (0.986)
    pallas_call x1, Pallas kernels: 69.1 us -> 68.4 us  [per_device(): pl.pallas_call(kernel, out_shape=jax.ShapeDtypeStruct((OWNED, hidden), bf...]
where the time goes in v3:
time: 72.8 us; the launch traced here: 72 us
  Pallas kernels  68.4 us (94%)
  matrix products  2.91 us (4%)
  between operations  0.74 us (1%)
    pallas_call x1, Pallas kernels, per_device(): pl.pallas_call(kernel, out_shape=jax.ShapeDtypeStruct((OWNED, hidden), bf...  68.4 us
    dot_general x1, matrix products, per_device(): jnp.dot(activated, w_second, preferred_element_type=jnp.float32) + b_second  2.91 us

profile of v3, /device:TPU:1, one launch (start us, length us, event | category | flops | bytes accessed | tf_op | source)
XLA Modules:
  0.0 72.0 jit_solution(5806979226359204842)
XLA Ops:
  0.0 0.0 copy-start
  0.7 0.0 copy-start.1
  0.7 68.4 %gin.1 = bf16[1024,512]{1,0:T(8,128)(2,1)} custom-call(s32[8,32]{1,0:T(8,128)} %bitcast.8, s32[1,32]{1,0:T(1,128)} %count_hbm.1, s32[24,64]{1,0:T(8,128)} %tile_hbm.1, f32[1]{0:T(128)S(6)} %copy.12.eps_ref, bf16[64,8192]{1,0:T(8,128)(2,1)} %feat_hbm.1, s32[24,8192]{1,0:T(8,128)} %near_hbm.1, s32[1,8192]{1,0:T(1,128)} %bitcast.7, bf16[512,512]{1,0:T(8,128)(2,1)} %w1_hbm.1, ...), custom_call_target="tpu_custom_call" | custom-call | tf_op jit(solution)/shard_map/gin/pallas_call | solution.py:363
  69.1 0.0 copy-done
  69.1 0.0 copy-done.1
  69.1 2.9 %add_convert_fusion = bf16[1024,512]{1,0:T(8,128)(2,1)} fusion(bf16[1024,512]{1,0:T(8,128)(2,1)} %gin.1, bf16[512,512]{1,0:T(8,128)(2,1)S(1)} %copy-done, f32[512]{0:T(512)S(1)} %copy-done.1), kind=kOutput, calls=%fused_computation | convolution fusion | flops 537919488 | bytes 2623488 | tf_op jit(solution)/shard_map/dot_general | solution.py:401
Async XLA Ops:
  0.0 69.1 %copy-start = (bf16[512,512]{1,0:T(8,128)(2,1)S(1)}, bf16[512,512]{1,0:T(8,128)(2,1)}, u32[]{:S(2)}) copy-start(bf16[512,512]{1,0:T(8,128)(2,1)} %param.20) | copy-start | bytes 1572868
  0.7 68.4 %copy-start.1 = (f32[512]{0:T(512)S(1)}, f32[512]{0:T(512)}, u32[]{:S(2)}) copy-start(f32[512]{0:T(512)} %param.21) | copy-start | bytes 6148
